TPU v7x, 32 devices: a whole 2x2x4 slice. The times are simulated.
32 devices in a mesh: groups: 2 (over y), block: 4 (over z), seg: 2 (over x), sub: 2 (over core).
Axes of the slice: x: 2, y: 2, z: 4, core: 2. Of those that a mesh axis runs over, the one named last changes fastest.
Arguments:
- old_fields: float32 [2048, 4, 512], P(('groups', 'block', 'seg', 'sub')), parts along dimension 0, may hold values from -6 to 6
- corner_shift: float32 [24, 2048], P(None, ('groups', 'block', 'seg', 'sub')), parts along dimension 1, may hold values from -0.2 to 0.2
- targets: float32 [3, 131072], P(None, ('groups', 'block', 'seg', 'sub')), parts along dimension 1, may hold values from -0.7 to 0.7
- owners: int32 [1024], P(('groups', 'block', 'seg', 'sub')), parts along dimension 0, may hold values from 0 to 1023, as said below
Outputs:
- new_fields: float32 [4, 131072], P(None, ('groups', 'block', 'seg', 'sub')), parts along dimension 1
There are 2 independent parts, one for each index of `groups`. A program takes and returns all parts, laid end to end along the dimension named above; each array names one. Nothing has to cross between parts.
Inputs may be any that keep to these rules, and one draw needn't show every extreme that they name: `owners`: owner e lies on device e // 64. At most 2 of the blocks on the rows of one device are owned by elements of any one device, and in every draw some device owns exactly 2 blocks of every device.
All inputs are finite; a program needn't handle non-finite values.
Results may differ from a plain program's by a relative error of at most 0.00029.
Values sent between devices are 32-bit elements; how exact they have to be, the bound alone decides.
A program may use at most 64 MiB of HBM per device.

v0:
```python
import jax
import jax.numpy as jnp
import numpy as np
from jax import lax
from jax.sharding import PartitionSpec as P

NEWTON = 3
CAP = 2
GLL_POINTS = (
    -1.0,
    -0.8717401485096066,
    -0.5917001814331423,
    -0.2092992179024789,
    0.2092992179024789,
    0.5917001814331423,
    0.8717401485096066,
    1.0,
)
EXACT = lax.Precision.HIGHEST


def lagrange_rows(coords):
    gll_nodes = jnp.array(GLL_POINTS, jnp.float32)
    offsets = coords[None, :] - gll_nodes[:, None]
    spacing = gll_nodes[:, None] - gll_nodes[None, :] + jnp.eye(8, dtype=jnp.float32)
    diag_mask = jnp.eye(8, dtype=bool)
    factors = jnp.where(diag_mask[:, :, None], 1.0, offsets[None, :, :] / spacing[:, :, None])
    return jnp.prod(factors, axis=1)


def corner_signs():
    bit_table = np.array(
        [[corner >> 2 - coord_dim & 1 for corner in range(8)] for coord_dim in range(3)], np.float32
    )
    return jnp.asarray(2.0 * bit_table - 1.0)


def outer_prod(first, second, third):
    return (first[:, None, None, :] * second[None, :, None, :] * third[None, None, :, :]).reshape(
        8, -1
    )


def trilinear(ref_pos):
    shape_list = []
    slope_list = []
    for coord_dim in range(3):
        coordinate = ref_pos[coord_dim]
        shape_list.append(jnp.stack([0.5 - 0.5 * coordinate, 0.5 + 0.5 * coordinate]))
        slope_list.append(
            jnp.stack([jnp.full_like(coordinate, -0.5), jnp.full_like(coordinate, 0.5)])
        )
    values = outer_prod(shape_list[0], shape_list[1], shape_list[2])
    slopes = [
        outer_prod(slope_list[0], shape_list[1], shape_list[2]),
        outer_prod(shape_list[0], slope_list[1], shape_list[2]),
        outer_prod(shape_list[0], shape_list[1], slope_list[2]),
    ]
    return (values, slopes)


def solve_three(matrix, rhs_rows):
    cofactors = []
    for row_id in range(3):
        keep_rows = [remain for remain in range(3) if remain != row_id]
        cof_row = []
        for col_id in range(3):
            keep_cols = [remain for remain in range(3) if remain != col_id]
            sign_factor = 1.0 if (row_id + col_id) % 2 == 0 else -1.0
            cof_row.append(
                sign_factor
                * (
                    matrix[keep_rows[0]][keep_cols[0]] * matrix[keep_rows[1]][keep_cols[1]]
                    - matrix[keep_rows[0]][keep_cols[1]] * matrix[keep_rows[1]][keep_cols[0]]
                )
            )
        cofactors.append(cof_row)
    determinant = (
        matrix[0][0] * cofactors[0][0]
        + matrix[0][1] * cofactors[0][1]
        + matrix[0][2] * cofactors[0][2]
    )
    return [
        (
            cofactors[0][col_id] * rhs_rows[0]
            + cofactors[1][col_id] * rhs_rows[1]
            + cofactors[2][col_id] * rhs_rows[2]
        )
        / determinant
        for col_id in range(3)
    ]


def invert_map(corners, target):
    ref_pos = jnp.zeros_like(target)
    for iteration in range(NEWTON):
        values, slopes = trilinear(ref_pos)
        mapped = jnp.dot(corners, values, precision=EXACT)
        columns = [jnp.dot(corners, slope_row, precision=EXACT) for slope_row in slopes]
        matrix = [[columns[col_id][row_id] for col_id in range(3)] for row_id in range(3)]
        misfit = mapped - target
        update = solve_three(matrix, [misfit[row_id] for row_id in range(3)])
        ref_pos = jnp.clip(ref_pos - jnp.stack(update), -1.2, 1.2)
    return ref_pos


def interpolate(element_field, corners, target):
    ref_pos = invert_map(corners, target)
    along_x = lagrange_rows(ref_pos[0])
    along_y = lagrange_rows(ref_pos[1])
    along_z = lagrange_rows(ref_pos[2])
    weights = (along_y[:, None, :] * along_z[None, :, :]).reshape(64, -1)
    var_count = element_field.shape[0]
    partial_sum = jnp.dot(element_field.reshape(var_count * 8, 64), weights, precision=EXACT)
    return jnp.sum(partial_sum.reshape(var_count, 8, -1) * along_x[None, :, :], axis=1)


def interpolate_blocks(fields, shifts, points):
    cube_signs = corner_signs()

    def per_block(inputs):
        element_field, shift_row, target = inputs
        return interpolate(element_field, cube_signs + shift_row.reshape(3, 8), target)

    return lax.map(per_block, (fields, shifts, points), batch_size=64)


def slot_table(owners, elems_local, capacity):
    owner_dev = owners // elems_local
    local_elem = owners - owner_dev * elems_local
    block_count = owners.shape[0]
    earlier = jnp.tril(jnp.ones((block_count, block_count), jnp.int32), -1)
    matches = (owner_dev[:, None] == owner_dev[None, :]).astype(jnp.int32)
    arrival = jnp.sum(matches * earlier, axis=1)
    return (owner_dev * capacity + arrival, local_elem)


def shards(old_fields, corner_shift, targets, owners):
    outer_count = lax.axis_size("block")
    inner_count = lax.axis_size("seg") * lax.axis_size("sub")
    slot_count = outer_count * inner_count * CAP
    elems_local = old_fields.shape[0]
    var_count = old_fields.shape[1]
    block_count = owners.shape[0]
    slot_index, local_elem = slot_table(owners, elems_local, CAP)
    block_points = targets.reshape(3, block_count, -1).transpose(1, 0, 2)
    point_count = block_points.shape[2]
    outgoing = jnp.zeros((slot_count, 3, point_count), jnp.float32).at[slot_index].set(block_points)
    wanted = jnp.full((slot_count,), -1, jnp.int32).at[slot_index].set(local_elem)
    arrived, asked = (
        lax.all_to_all(
            lax.all_to_all(
                outgoing.reshape(outer_count, inner_count, CAP, 3, point_count),
                "block",
                split_axis=0,
                concat_axis=0,
                tiled=True,
            ),
            ("seg", "sub"),
            split_axis=1,
            concat_axis=1,
            tiled=True,
        ),
        lax.all_to_all(
            lax.all_to_all(
                wanted.reshape(outer_count, inner_count, CAP),
                "block",
                split_axis=0,
                concat_axis=0,
                tiled=True,
            ),
            ("seg", "sub"),
            split_axis=1,
            concat_axis=1,
            tiled=True,
        ),
    )
    asked = asked.reshape(slot_count)
    live_slot = asked >= 0
    element = jnp.where(live_slot, asked, 0)
    fields = old_fields[element]
    shifts = jnp.transpose(corner_shift[:, element])
    computed = interpolate_blocks(fields, shifts, arrived.reshape(slot_count, 3, point_count))
    computed = jnp.where(live_slot[:, None, None], computed, 0.0)
    returned = lax.all_to_all(
        lax.all_to_all(
            computed.reshape(outer_count, inner_count, CAP, var_count, point_count),
            "block",
            split_axis=0,
            concat_axis=0,
            tiled=True,
        ),
        ("seg", "sub"),
        split_axis=1,
        concat_axis=1,
        tiled=True,
    )
    mine = returned.reshape(slot_count, var_count, point_count)[slot_index]
    return mine.transpose(1, 0, 2).reshape(var_count, -1)


def solution(mesh):
    in_specs = (
        P(("groups", "block", "seg", "sub"), None, None),
        P(None, ("groups", "block", "seg", "sub")),
        P(None, ("groups", "block", "seg", "sub")),
        P(("groups", "block", "seg", "sub")),
    )
    out_specs = P(None, ("groups", "block", "seg", "sub"))
    return jax.shard_map(shards, mesh=mesh, in_specs=in_specs, out_specs=out_specs, check_vma=False)
```

profile of v0, /device:TPU:0, one launch (start us, length us, event | category | flops | bytes accessed | tf_op | source)
XLA Modules:
  0.0 64.6 jit_solution(12692678252523733216)
XLA Ops:
  0.0 0.7 %multiply_subtract_fusion.2 = (s32[32]{0:T(128)S(1)}, s32[32]{0:T(128)S(1)}, s32[32]{0:T(128)S(1)}) fusion(s32[32]{0:T(128)} %param.11), kind=kLoop, calls=%fused_computation.237 | loop fusion | flops 576 | bytes 512 | tf_op jit(solution)/shard_map/sub | solution.py:130
  0.7 0.2 select_reduce_fusion
  0.9 0.7 %scatter_custom_fusion = s32[32]{0:T(128)S(1)} fusion(s32[32]{0:T(128)S(1)} %compare_select_fusion.2, s32[32]{0:T(128)S(1)} %get-tuple-element.10, s32[]{:T(128)} %constant.26.clone.1), kind=kCustom, calls=%fused_computation.239 | custom fusion | bytes 132 | tf_op jit(solution)/shard_map/scatter | solution.py:149
  1.7 0.7 %copy.272 = s32[4,4,2]{1,2,0:T(2,128)} copy(s32[4,4,2]{2,1,0:T(4,128)S(1)} %reshape.2161) | data formatting | bytes 256 | tf_op jit(solution)/shard_map/reshape | solution.py:166
  2.4 6.5 %all-to-all-start = ((s32[4,4,2]{1,2,0:T(2,128)}), s32[4,4,2]{1,2,0:T(2,128)S(1)}, u32[]{:S(2)}, u32[]{:S(2)}) async-start(s32[4,4,2]{1,2,0:T(2,128)} %copy.272), calls=%async_computation | async-start | bytes 8192 | tf_op jit(solution)/shard_map/all_to_all | solution.py:165
  9.1 1.5 %scatter_fusion = f32[32,3,128]{2,1,0:T(4,128)S(1)} fusion(f32[32,3,128]{2,1,0:T(4,128)S(1)} %broadcast.569, s32[32]{0:T(128)S(1)} %compare_select_fusion.2, f32[32,3,128]{2,1,0:T(4,128)S(1)} %bitcast.790), kind=kCustom, calls=%fused_computation.4 | custom fusion | bytes 147584 | tf_op jit(solution)/shard_map/scatter | solution.py:148
  10.6 3.9 %all-to-all-done = s32[4,4,2]{1,2,0:T(2,128)S(1)} async-done(((s32[4,4,2]{1,2,0:T(2,128)}), s32[4,4,2]{1,2,0:T(2,128)S(1)}, u32[]{:S(2)}, u32[]{:S(2)}) %all-to-all-start) | async-done | bytes 160 | tf_op jit(solution)/shard_map/all_to_all | solution.py:165
  14.5 0.7 %copy.273 = s32[4,4,2]{0,2,1:T(2,128)} copy(s32[4,4,2]{1,2,0:T(2,128)S(1)} %all-to-all-done) | data formatting | bytes 256 | tf_op jit(solution)/shard_map/all_to_all | solution.py:165
  15.2 3.2 %all-to-all-start.1 = ((s32[4,4,2]{0,2,1:T(2,128)}), s32[4,4,2]{0,2,1:T(2,128)S(1)}, u32[]{:S(2)}, u32[]{:S(2)}) async-start(s32[4,4,2]{0,2,1:T(2,128)} %copy.273), calls=%async_computation.1 | async-start | bytes 8192 | tf_op jit(solution)/shard_map/all_to_all | solution.py:164
  18.4 0.6 %copy.281 = f32[4,4,2,3,128]{4,2,1,3,0:T(2,128)} copy(f32[4,4,2,3,128]{4,3,2,1,0:T(4,128)S(1)} %bitcast.767) | data formatting | bytes 98304 | tf_op jit(solution)/shard_map/reshape | solution.py:153
  19.1 3.1 %all-to-all-done.1 = s32[4,4,2]{0,2,1:T(2,128)S(1)} async-done(((s32[4,4,2]{0,2,1:T(2,128)}), s32[4,4,2]{0,2,1:T(2,128)S(1)}, u32[]{:S(2)}, u32[]{:S(2)}) %all-to-all-start.1) | async-done | bytes 160 | tf_op jit(solution)/shard_map/all_to_all | solution.py:164
  22.2 3.3 %all-to-all-start.2 = ((f32[4,4,2,3,128]{4,2,1,3,0:T(2,128)}), f32[4,4,2,3,128]{4,2,1,3,0:T(2,128)S(1)}, u32[]{:S(2)}, u32[]{:S(2)}) async-start(f32[4,4,2,3,128]{4,2,1,3,0:T(2,128)} %copy.281), calls=%async_computation.2 | async-start | bytes 98304 | tf_op jit(solution)/shard_map/all_to_all | solution.py:152
  25.5 0.1 copy.276
  25.6 0.1 reshape.2162
  25.7 0.6 gather_fusion.1
  26.3 0.6 copy-done.4
  26.9 0.7 %copy-done.6 = f32[24]{0:T(128)S(1)} copy-done((f32[24]{0:T(128)S(1)}, f32[24]{0:T(128)}, u32[]{:S(2)}) %copy-start.6) | copy-done | bytes 120
  27.6 0.3 fusion.91
  27.9 0.3 fusion.93
  28.3 0.3 fusion.95
  28.6 0.3 copy-done.5
  29.1 0.1 copy.274
  29.1 2.0 %all-to-all-done.2 = f32[4,4,2,3,128]{4,2,1,3,0:T(2,128)S(1)} async-done(((f32[4,4,2,3,128]{4,2,1,3,0:T(2,128)}), f32[4,4,2,3,128]{4,2,1,3,0:T(2,128)S(1)}, u32[]{:S(2)}, u32[]{:S(2)}) %all-to-all-start.2) | async-done | bytes 49184 | tf_op jit(solution)/shard_map/all_to_all | solution.py:152
  31.1 0.6 copy.282
  31.8 3.3 %all-to-all-start.3 = ((f32[4,4,2,3,128]{4,2,0,3,1:T(2,128)}), f32[4,4,2,3,128]{4,2,0,3,1:T(2,128)S(1)}, u32[]{:S(2)}, u32[]{:S(2)}) async-start(f32[4,4,2,3,128]{4,2,0,3,1:T(2,128)} %copy.282), calls=%async_computation.3 | async-start | bytes 98304 | tf_op jit(solution)/shard_map/all_to_all | solution.py:151
  35.2 0.7 %gather_fusion = f32[32,4,512]{2,1,0:T(4,128)S(1)} fusion(f32[64,4,512]{2,1,0:T(4,128)S(1)} %copy-done, s32[1024]{0:T(1024)S(1)} %pad_clamp_fusion.1), kind=kCustom, calls=%fused_computation | custom fusion | bytes 524416 | tf_op jit(solution)/shard_map/gather | solution.py:181
  35.9 0.2 reshape.2163
  36.1 0.1 copy.275
  36.2 2.8 %all-to-all-done.3 = f32[4,4,2,3,128]{4,2,0,3,1:T(2,128)S(1)} async-done(((f32[4,4,2,3,128]{4,2,0,3,1:T(2,128)}), f32[4,4,2,3,128]{4,2,0,3,1:T(2,128)S(1)}, u32[]{:S(2)}, u32[]{:S(2)}) %all-to-all-start.3) | async-done | bytes 49184 | tf_op jit(solution)/shard_map/all_to_all | solution.py:151
  39.1 0.3 convolution_subtract_fusion
  39.7 0.6 copy-done.2
  40.5 0.3 fusion.23
  40.9 0.3 fusion.17
  41.4 0.3 fusion.19
  41.7 0.3 fusion.21
  42.5 0.3 fusion.13
  42.9 0.3 fusion.11
  43.3 0.3 fusion.15
  43.7 0.3 fusion.9
  44.3 0.1 broadcast_add_fusion.2
  44.4 1.1 %fusion.4 = (f32[32,8,128]{2,1,0:T(8,128)S(1)}, f32[32,8,128]{2,1,0:T(8,128)S(1)}, f32[32,8,128]{2,1,0:T(8,128)S(1)}) fusion(f32[32,8,128]{2,1,0:T(8,128)S(1)} %get-tuple-element.61, f32[8,8]{1,0:T(8,128)S(1)} %add_add_fusion, pred[8,8]{1,0:T(8,128)(4,1)S(1)} %iota_compare_fusion.1, f32[32,8,128]{2,1,0:T(8,128)S(1)} %get-tuple-element.60, ...), kind=kLoop, calls=%fused_computation.14 | loop fusion | flops 2260992 | bytes 786752 | tf_op jit(solution)/shard_map/vmap()/reduce_prod | solution.py:28
  45.4 1.1 %fusion.1 = f32[32,4,128]{2,1,0:T(4,128)S(1)} fusion(f32[32,32,64]{2,1,0:T(8,128)S(1)} %reshape.2163, f32[32,8,128]{2,1,0:T(8,128)S(1)} %get-tuple-element.6, f32[32,8,128]{2,1,0:T(8,128)S(1)} %get-tuple-element.7, f32[32,8,128]{2,1,0:T(8,128)S(1)} %get-tuple-element.5), kind=kOutput, calls=%fused_computation.7 | convolution fusion | flops 101171200 | bytes 720896 | tf_op jit(solution)/shard_map/vmap()/dot_general | solution.py:114
  46.6 0.1 broadcast_select_fusion
  46.7 8.6 %all_to_all.30 = f32[4,4,2,4,128]{4,2,1,3,0:T(2,128)S(1)} all-to-all(f32[4,4,2,4,128]{4,2,1,3,0:T(2,128)S(1)} %copy.319), channel_id=1, replica_groups=mesh['groups'=2,'block'=4,'seg'=2,'sub'=2] {'block'}, dimensions={0} | all-to-all | bytes 131072 | tf_op jit(solution)/shard_map/all_to_all | solution.py:186
  55.3 0.6 %copy.320 = f32[4,4,2,4,128]{4,3,2,0,1:T(4,128)} copy(f32[4,4,2,4,128]{4,2,1,3,0:T(2,128)S(1)} %all_to_all.30) | data formatting | bytes 131072 | tf_op jit(solution)/shard_map/all_to_all | solution.py:186
  56.0 3.3 %all-to-all-start.5 = ((f32[4,4,2,4,128]{4,3,2,0,1:T(4,128)}), f32[4,4,2,4,128]{4,3,2,0,1:T(4,128)S(1)}, u32[]{:S(2)}, u32[]{:S(2)}) async-start(f32[4,4,2,4,128]{4,3,2,0,1:T(4,128)} %copy.320), calls=%async_computation.5 | async-start | bytes 131072 | tf_op jit(solution)/shard_map/all_to_all | solution.py:185
  59.3 4.1 %all-to-all-done.5 = f32[4,4,2,4,128]{4,3,2,0,1:T(4,128)S(1)} async-done(((f32[4,4,2,4,128]{4,3,2,0,1:T(4,128)}), f32[4,4,2,4,128]{4,3,2,0,1:T(4,128)S(1)}, u32[]{:S(2)}, u32[]{:S(2)}) %all-to-all-start.5) | async-done | bytes 65568 | tf_op jit(solution)/shard_map/all_to_all | solution.py:185
  63.4 1.2 %gather_fusion.2 = f32[32,4,128]{2,1,0:T(4,128)} fusion(f32[32,4,128]{2,1,0:T(4,128)S(1)} %bitcast.769, s32[1024]{0:T(1024)S(1)} %pad_clamp_fusion), kind=kCustom, calls=%fused_computation.2 | custom fusion | bytes 131200 | tf_op jit(solution)/shard_map/gather | solution.py:198
  (75 shorter events, 1.7 us)
Async XLA Ops:
  0.0 35.1 %copy-start = (f32[64,4,512]{2,1,0:T(4,128)S(1)}, f32[64,4,512]{2,1,0:T(4,128)}, u32[]{:S(2)}) copy-start(f32[64,4,512]{2,1,0:T(4,128)} %param.8) | copy-start | bytes 1572868
  1.7 7.2 %copy-start.3 = (f32[24,64]{1,0:T(8,128)S(1)}, f32[24,64]{1,0:T(8,128)}, u32[]{:S(2)}) copy-start(f32[24,64]{1,0:T(8,128)} %param.9) | copy-start | bytes 18436
  1.7 7.3 %copy-start.7 = (f32[8]{0:T(128)S(1)}, f32[8]{0:T(128)}, u32[]{:S(2)}) copy-start(f32[8]{0:T(128)} %constant.77) | copy-start | bytes 100
  1.7 7.3 %copy-start.8 = (f32[8]{0:T(128)S(1)}, f32[8]{0:T(128)}, u32[]{:S(2)}) copy-start(f32[8]{0:T(128)} %constant.75.clone) | copy-start | bytes 100
  2.4 6.7 %copy-start.1 = (f32[3,4096]{1,0:T(4,128)S(1)}, f32[3,4096]{1,0:T(4,128)}, u32[]{:S(2)}) copy-start(f32[3,4096]{1,0:T(4,128)} %param.10) | copy-start | bytes 147460
  2.4 12.1 %all-to-all-start = ((s32[4,4,2]{1,2,0:T(2,128)}), s32[4,4,2]{1,2,0:T(2,128)S(1)}, u32[]{:S(2)}, u32[]{:S(2)}) async-start(s32[4,4,2]{1,2,0:T(2,128)} %copy.272), calls=%async_computation | async-start | bytes 8192 | tf_op jit(solution)/shard_map/all_to_all | solution.py:165
  15.2 7.0 %all-to-all-start.1 = ((s32[4,4,2]{0,2,1:T(2,128)}), s32[4,4,2]{0,2,1:T(2,128)S(1)}, u32[]{:S(2)}, u32[]{:S(2)}) async-start(s32[4,4,2]{0,2,1:T(2,128)} %copy.273), calls=%async_computation.1 | async-start | bytes 8192 | tf_op jit(solution)/shard_map/all_to_all | solution.py:164
  22.2 8.9 %all-to-all-start.2 = ((f32[4,4,2,3,128]{4,2,1,3,0:T(2,128)}), f32[4,4,2,3,128]{4,2,1,3,0:T(2,128)S(1)}, u32[]{:S(2)}, u32[]{:S(2)}) async-start(f32[4,4,2,3,128]{4,2,1,3,0:T(2,128)} %copy.281), calls=%async_computation.2 | async-start | bytes 98304 | tf_op jit(solution)/shard_map/all_to_all | solution.py:152
  26.3 0.7 %copy-start.4 = (f32[2,128]{1,0:T(2,128)S(1)}, f32[2,128]{1,0:T(2,128)}, u32[]{:S(2)}) copy-start(f32[2,128]{1,0:T(2,128)} %constant.68.clone.1) | copy-start | bytes 3076
  26.9 0.7 %copy-start.6 = (f32[24]{0:T(128)S(1)}, f32[24]{0:T(128)}, u32[]{:S(2)}) copy-start(f32[24]{0:T(128)} %constant.76) | copy-start | bytes 292
  28.3 0.7 %copy-start.5 = (f32[3,8]{1,0:T(4,128)S(1)}, f32[3,8]{1,0:T(4,128)}, u32[]{:S(2)}) copy-start(f32[3,8]{1,0:T(4,128)} %constant.74.clone) | copy-start | bytes 292
  31.8 7.3 %all-to-all-start.3 = ((f32[4,4,2,3,128]{4,2,0,3,1:T(2,128)}), f32[4,4,2,3,128]{4,2,0,3,1:T(2,128)S(1)}, u32[]{:S(2)}, u32[]{:S(2)}) async-start(f32[4,4,2,3,128]{4,2,0,3,1:T(2,128)} %copy.282), calls=%async_computation.3 | async-start | bytes 98304 | tf_op jit(solution)/shard_map/all_to_all | solution.py:151
  39.6 0.7 %copy-start.2 = (f32[2,128]{1,0:T(2,128)S(1)}, f32[2,128]{1,0:T(2,128)}, u32[]{:S(2)}) copy-start(f32[2,128]{1,0:T(2,128)} %constant.73.clone.1) | copy-start | bytes 3076
  56.0 7.4 %all-to-all-start.5 = ((f32[4,4,2,4,128]{4,3,2,0,1:T(4,128)}), f32[4,4,2,4,128]{4,3,2,0,1:T(4,128)S(1)}, u32[]{:S(2)}, u32[]{:S(2)}) async-start(f32[4,4,2,4,128]{4,3,2,0,1:T(4,128)} %copy.320), calls=%async_computation.5 | async-start | bytes 131072 | tf_op jit(solution)/shard_map/all_to_all | solution.py:185
where the time goes:
time: 65.3 us; the launch traced here: 64.6 us
  starting transfers between devices  19.6 us (30%)
  waiting for transfers between devices  15.9 us (24%)
  local copies, waits for them, and re-layouts  12 us (18%)
  blocking collectives  8.63 us (13%)
  matrix products  5.16 us (8%)
  other arithmetic  2.71 us (4%)
    all_to_all x1, blocking collectives, shards(): lax.all_to_all(computed.reshape(outer_count, inner_count, CAP, var_count,...  8.63 us
    all_to_all x1, starting transfers between devices, shards(): lax.all_to_all(wanted.reshape(outer_count, inner_count, CAP), 'block', sp...  6.48 us
    all_to_all x1, waiting for transfers between devices, shards(): lax.all_to_all(lax.all_to_all(computed.reshape(outer_count, inner_count,...  4.07 us
    all_to_all x1, waiting for transfers between devices, shards(): lax.all_to_all(wanted.reshape(outer_count, inner_count, CAP), 'block', sp...  3.88 us
    all_to_all x1, starting transfers between devices, shards(): lax.all_to_all(lax.all_to_all(computed.reshape(outer_count, inner_count,...  3.28 us
    all_to_all x1, starting transfers between devices, shards(): lax.all_to_all(outgoing.reshape(outer_count, inner_count, CAP, 3, point_c...  3.27 us
    all_to_all x1, starting transfers between devices, shards(): lax.all_to_all(lax.all_to_all(outgoing.reshape(outer_count, inner_count,...  3.27 us
    all_to_all x1, starting transfers between devices, shards(): lax.all_to_all(lax.all_to_all(wanted.reshape(outer_count, inner_count, CA...  3.24 us
  transfers between devices with their start and end apart: 5, of which 5 were waited for; matrix products, arithmetic and copies ran while one was open for 8% of the time, Pallas kernels for 0%

commit v1 on v0

--- a/solution.py
+++ b/solution.py
@@ -1,3 +1,4 @@
+import functools
 import jax
 import jax.numpy as jnp
 import numpy as np
@@ -17,6 +18,44 @@
     1.0,
 )
 EXACT = lax.Precision.HIGHEST
+
+
+def boxes_use(block_here, array_axis, frame):
+    wide_out, clean = (block_here.shape[:array_axis], block_here.shape[array_axis + 1 :])
+    value_now = block_here.reshape(*wide_out, frame, -1, *clean)
+    return jnp.moveaxis(value_now, array_axis, 0)
+
+
+def guide_windows_in(block_in, axis_no):
+    placed = list(block_in.shape[1:])
+    placed[axis_no] *= block_in.shape[0]
+    return jnp.moveaxis(block_in, 0, axis_no).reshape(placed)
+
+
+def digits_supply(sample, bus_axis, vector, local_array):
+    formed = jax.lax.axis_size(bus_axis)
+    raw_out = jax.lax.axis_index(bus_axis)
+    current_block, o_now = (formed, raw_out)
+    e_next = boxes_use(sample, vector, current_block)
+    v1 = e_next
+    pp = 1
+    while pp < current_block:
+        then, f_now = ((o_now + pp) % current_block, (o_now - pp) % current_block)
+        met_up = lax.dynamic_index_in_dim(e_next, then, 0)
+        lanes = []
+        p = 0
+        while p < current_block:
+            lanes.append((p, (p + pp) % current_block))
+            p = p + 1
+        even = jax.lax.ppermute(met_up, bus_axis, lanes)
+        v1 = lax.dynamic_update_slice_in_dim(v1, even, f_now, axis=0)
+        pp += 1
+    return guide_windows_in(v1, local_array)
+
+
+resolve_skins_on = functools.partial(
+    digits_supply, bus_axis=("seg", "sub"), vector=1, local_array=1
+)
 
 
 def lagrange_rows(coords):
@@ -182,18 +221,14 @@
     shifts = jnp.transpose(corner_shift[:, element])
     computed = interpolate_blocks(fields, shifts, arrived.reshape(slot_count, 3, point_count))
     computed = jnp.where(live_slot[:, None, None], computed, 0.0)
-    returned = lax.all_to_all(
+    returned = resolve_skins_on(
         lax.all_to_all(
             computed.reshape(outer_count, inner_count, CAP, var_count, point_count),
             "block",
             split_axis=0,
             concat_axis=0,
             tiled=True,
-        ),
-        ("seg", "sub"),
-        split_axis=1,
-        concat_axis=1,
-        tiled=True,
+        )
     )
     mine = returned.reshape(slot_count, var_count, point_count)[slot_index]
     return mine.transpose(1, 0, 2).reshape(var_count, -1)

time: 65.3 us -> 62.7 us (0.960)
  blocking collectives: 8.63 us -> 0 us
  waiting for transfers between devices: 15.9 us -> 19.5 us
  starting transfers between devices: 19.6 us -> 21.3 us
    all_to_all x1 -> x0, blocking collectives: 8.63 us -> none  [shards(): lax.all_to_all(computed.reshape(outer_count, inner_count, CAP, var_count,...]
    ppermute x0 -> x3, waiting for transfers between devices: none -> 2.08 us  [digits_supply(): even = jax.lax.ppermute(met_up, bus_axis, lanes)]
    ppermute x0 -> x3, starting transfers between devices: none -> 1.78 us  [digits_supply(): even = jax.lax.ppermute(met_up, bus_axis, lanes)]
    all_to_all x1, waiting for transfers between devices: 4.07 us -> 5.67 us  [shards(): lax.all_to_all(computed.reshape(outer_count, inner_count, CAP, var_count,...]
  transfers between devices with their start and end apart: 5 -> 8, of which waited for: 5 -> 7; matrix products, arithmetic and copies ran while one was open for 8% -> 9% of each run, Pallas kernels for 0% -> 0%
where the time goes in v1:
time: 62.7 us; the launch traced here: 61.5 us
  starting transfers between devices  21.3 us (34%)
  waiting for transfers between devices  19.5 us (31%)
  local copies, waits for them, and re-layouts  11.4 us (18%)
  matrix products  5.16 us (8%)
  other arithmetic  3.36 us (5%)
  between operations  0.73 us (1%)
    all_to_all x1, starting transfers between devices, shards(): lax.all_to_all(wanted.reshape(outer_count, inner_count, CAP), 'block', sp...  6.48 us
    all_to_all x1, waiting for transfers between devices, shards(): lax.all_to_all(computed.reshape(outer_count, inner_count, CAP, var_count,...  5.67 us
    all_to_all x1, waiting for transfers between devices, shards(): lax.all_to_all(wanted.reshape(outer_count, inner_count, CAP), 'block', sp...  3.88 us
    all_to_all x1, starting transfers between devices, shards(): lax.all_to_all(computed.reshape(outer_count, inner_count, CAP, var_count,...  3.28 us
    all_to_all x1, starting transfers between devices, shards(): lax.all_to_all(outgoing.reshape(outer_count, inner_count, CAP, 3, point_c...  3.27 us
    all_to_all x1, starting transfers between devices, shards(): lax.all_to_all(lax.all_to_all(outgoing.reshape(outer_count, inner_count,...  3.27 us
    all_to_all x1, starting transfers between devices, shards(): lax.all_to_all(lax.all_to_all(wanted.reshape(outer_count, inner_count, CA...  3.2 us
    all_to_all x1, waiting for transfers between devices, shards(): lax.all_to_all(lax.all_to_all(wanted.reshape(outer_count, inner_count, CA...  3.11 us
  transfers between devices with their start and end apart: 8, of which 7 were waited for; matrix products, arithmetic and copies ran while one was open for 9% of the time, Pallas kernels for 0%

profile of v1, /device:TPU:0, one launch (start us, length us, event | category | flops | bytes accessed | tf_op | source)
XLA Modules:
  0.0 61.5 jit_solution(679950996878149628)
XLA Ops:
  0.0 0.7 %multiply_subtract_fusion.2 = (s32[32]{0:T(128)S(1)}, s32[32]{0:T(128)S(1)}, s32[32]{0:T(128)S(1)}) fusion(s32[32]{0:T(128)} %param.11), kind=kLoop, calls=%fused_computation.243 | loop fusion | flops 576 | bytes 512 | tf_op jit(solution)/shard_map/sub | solution.py:169
  0.7 0.2 select_reduce_fusion
  0.9 0.7 %scatter_custom_fusion = s32[32]{0:T(128)S(1)} fusion(s32[32]{0:T(128)S(1)} %compare_select_fusion.2, s32[32]{0:T(128)S(1)} %get-tuple-element.10, s32[]{:T(128)} %constant.106.clone.1), kind=kCustom, calls=%fused_computation.245 | custom fusion | bytes 132 | tf_op jit(solution)/shard_map/scatter | solution.py:188
  1.7 0.7 %copy.171 = s32[4,4,2]{1,2,0:T(2,128)} copy(s32[4,4,2]{2,1,0:T(4,128)S(1)} %reshape.2170) | data formatting | bytes 256 | tf_op jit(solution)/shard_map/reshape | solution.py:205
  2.4 6.5 %all-to-all-start = ((s32[4,4,2]{1,2,0:T(2,128)}), s32[4,4,2]{1,2,0:T(2,128)S(1)}, u32[]{:S(2)}, u32[]{:S(2)}) async-start(s32[4,4,2]{1,2,0:T(2,128)} %copy.171), calls=%async_computation | async-start | bytes 8192 | tf_op jit(solution)/shard_map/all_to_all | solution.py:204
  9.1 1.5 %scatter_fusion = f32[32,3,128]{2,1,0:T(4,128)S(1)} fusion(f32[32,3,128]{2,1,0:T(4,128)S(1)} %broadcast.575, s32[32]{0:T(128)S(1)} %compare_select_fusion.2, f32[32,3,128]{2,1,0:T(4,128)S(1)} %bitcast.802), kind=kCustom, calls=%fused_computation.4 | custom fusion | bytes 147584 | tf_op jit(solution)/shard_map/scatter | solution.py:187
  10.6 3.9 %all-to-all-done = s32[4,4,2]{1,2,0:T(2,128)S(1)} async-done(((s32[4,4,2]{1,2,0:T(2,128)}), s32[4,4,2]{1,2,0:T(2,128)S(1)}, u32[]{:S(2)}, u32[]{:S(2)}) %all-to-all-start) | async-done | bytes 160 | tf_op jit(solution)/shard_map/all_to_all | solution.py:204
  14.5 0.7 %copy.172 = s32[4,4,2]{0,2,1:T(2,128)} copy(s32[4,4,2]{1,2,0:T(2,128)S(1)} %all-to-all-done) | data formatting | bytes 256 | tf_op jit(solution)/shard_map/all_to_all | solution.py:204
  15.2 3.2 %all-to-all-start.1 = ((s32[4,4,2]{0,2,1:T(2,128)}), s32[4,4,2]{0,2,1:T(2,128)S(1)}, u32[]{:S(2)}, u32[]{:S(2)}) async-start(s32[4,4,2]{0,2,1:T(2,128)} %copy.172), calls=%async_computation.1 | async-start | bytes 8192 | tf_op jit(solution)/shard_map/all_to_all | solution.py:203
  18.4 0.6 %copy.180 = f32[4,4,2,3,128]{4,2,1,3,0:T(2,128)} copy(f32[4,4,2,3,128]{4,3,2,1,0:T(4,128)S(1)} %bitcast.780) | data formatting | bytes 98304 | tf_op jit(solution)/shard_map/reshape | solution.py:192
  19.0 3.1 %all-to-all-done.1 = s32[4,4,2]{0,2,1:T(2,128)S(1)} async-done(((s32[4,4,2]{0,2,1:T(2,128)}), s32[4,4,2]{0,2,1:T(2,128)S(1)}, u32[]{:S(2)}, u32[]{:S(2)}) %all-to-all-start.1) | async-done | bytes 160 | tf_op jit(solution)/shard_map/all_to_all | solution.py:203
  22.1 3.3 %all-to-all-start.2 = ((f32[4,4,2,3,128]{4,2,1,3,0:T(2,128)}), f32[4,4,2,3,128]{4,2,1,3,0:T(2,128)S(1)}, u32[]{:S(2)}, u32[]{:S(2)}) async-start(f32[4,4,2,3,128]{4,2,1,3,0:T(2,128)} %copy.180), calls=%async_computation.2 | async-start | bytes 98304 | tf_op jit(solution)/shard_map/all_to_all | solution.py:191
  25.4 0.1 copy.175
  25.6 0.6 gather_fusion.1
  26.3 0.6 copy-done.4
  26.9 0.7 %copy-done.6 = f32[24]{0:T(128)S(1)} copy-done((f32[24]{0:T(128)S(1)}, f32[24]{0:T(128)}, u32[]{:S(2)}) %copy-start.6) | copy-done | bytes 120
  27.6 0.3 fusion.91
  27.9 0.3 fusion.93
  28.3 0.3 fusion.95
  28.6 0.3 copy-done.5
  29.0 0.1 copy.173
  29.1 2.0 %all-to-all-done.2 = f32[4,4,2,3,128]{4,2,1,3,0:T(2,128)S(1)} async-done(((f32[4,4,2,3,128]{4,2,1,3,0:T(2,128)}), f32[4,4,2,3,128]{4,2,1,3,0:T(2,128)S(1)}, u32[]{:S(2)}, u32[]{:S(2)}) %all-to-all-start.2) | async-done | bytes 49184 | tf_op jit(solution)/shard_map/all_to_all | solution.py:191
  31.1 0.6 %copy.181 = f32[4,4,2,3,128]{4,2,0,3,1:T(2,128)} copy(f32[4,4,2,3,128]{4,2,1,3,0:T(2,128)S(1)} %all-to-all-done.2) | data formatting | bytes 98304 | tf_op jit(solution)/shard_map/all_to_all | solution.py:191
  31.7 3.3 %all-to-all-start.3 = ((f32[4,4,2,3,128]{4,2,0,3,1:T(2,128)}), f32[4,4,2,3,128]{4,2,0,3,1:T(2,128)S(1)}, u32[]{:S(2)}, u32[]{:S(2)}) async-start(f32[4,4,2,3,128]{4,2,0,3,1:T(2,128)} %copy.181), calls=%async_computation.3 | async-start | bytes 98304 | tf_op jit(solution)/shard_map/all_to_all | solution.py:190
  35.1 0.7 %gather_fusion = f32[32,4,512]{2,1,0:T(4,128)S(1)} fusion(f32[64,4,512]{2,1,0:T(4,128)S(1)} %copy-done, s32[1024]{0:T(1024)S(1)} %pad_clamp_fusion.1), kind=kCustom, calls=%fused_computation | custom fusion | bytes 524416 | tf_op jit(solution)/shard_map/gather | solution.py:220
  35.8 0.2 reshape.2172
  36.0 0.1 copy.174
  36.2 2.8 %all-to-all-done.3 = f32[4,4,2,3,128]{4,2,0,3,1:T(2,128)S(1)} async-done(((f32[4,4,2,3,128]{4,2,0,3,1:T(2,128)}), f32[4,4,2,3,128]{4,2,0,3,1:T(2,128)S(1)}, u32[]{:S(2)}, u32[]{:S(2)}) %all-to-all-start.3) | async-done | bytes 49184 | tf_op jit(solution)/shard_map/all_to_all | solution.py:190
  39.0 0.3 convolution_subtract_fusion
  39.6 0.6 %copy-done.2 = f32[2,128]{1,0:T(2,128)S(1)} copy-done((f32[2,128]{1,0:T(2,128)S(1)}, f32[2,128]{1,0:T(2,128)}, u32[]{:S(2)}) %copy-start.2) | copy-done | bytes 1048
  40.4 0.3 fusion.23
  40.9 0.3 fusion.17
  41.3 0.3 fusion.19
  41.7 0.3 fusion.21
  42.4 0.3 fusion.13
  42.8 0.3 fusion.11
  43.2 0.3 fusion.15
  43.7 0.3 fusion.9
  44.3 1.1 %fusion.4 = (f32[32,8,128]{2,1,0:T(8,128)S(1)}, f32[32,8,128]{2,1,0:T(8,128)S(1)}, f32[32,8,128]{2,1,0:T(8,128)S(1)}) fusion(f32[32,8,128]{2,1,0:T(8,128)S(1)} %get-tuple-element.64, f32[8,8]{1,0:T(8,128)S(1)} %add_add_fusion, pred[8,8]{1,0:T(8,128)(4,1)S(1)} %iota_compare_fusion.1, f32[32,8,128]{2,1,0:T(8,128)S(1)} %get-tuple-element.63, ...), kind=kLoop, calls=%fused_computation.14 | loop fusion | flops 2260992 | bytes 786752 | tf_op jit(solution)/shard_map/vmap()/reduce_prod | solution.py:67
  45.4 1.1 %fusion.1 = f32[32,4,128]{2,1,0:T(4,128)S(1)} fusion(f32[32,32,64]{2,1,0:T(8,128)S(1)} %reshape.2172, f32[32,8,128]{2,1,0:T(8,128)S(1)} %get-tuple-element.6, f32[32,8,128]{2,1,0:T(8,128)S(1)} %get-tuple-element.7, f32[32,8,128]{2,1,0:T(8,128)S(1)} %get-tuple-element.5), kind=kOutput, calls=%fused_computation.7 | convolution fusion | flops 101171200 | bytes 720896 | tf_op jit(solution)/shard_map/vmap()/dot_general | solution.py:153
  46.5 0.7 %broadcast_select_fusion = f32[4,4,2,4,128]{4,3,2,1,0:T(4,128)} fusion(f32[4,4,2,4,128]{4,3,2,1,0:T(4,128)S(1)} %bitcast.781, pred[4,4,2]{2,1,0:T(4,128)(4,1)S(1)} %copy.174), kind=kLoop, calls=%fused_computation.57 | loop fusion | flops 16384 | bytes 131104 | tf_op jit(solution)/shard_map/jit(_where)/select_n | solution.py:223
  47.3 3.3 %all-to-all-start.4 = ((f32[4,4,2,4,128]{4,3,2,1,0:T(4,128)}), f32[4,4,2,4,128]{4,3,2,1,0:T(4,128)S(1)}, u32[]{:S(2)}, u32[]{:S(2)}) async-start(f32[4,4,2,4,128]{4,3,2,1,0:T(4,128)} %broadcast_select_fusion), calls=%async_computation.4 | async-start | bytes 131072 | tf_op jit(solution)/shard_map/all_to_all | solution.py:225
  50.6 5.7 %all-to-all-done.4 = f32[4,4,2,4,128]{4,3,2,1,0:T(4,128)S(1)} async-done(((f32[4,4,2,4,128]{4,3,2,1,0:T(4,128)}), f32[4,4,2,4,128]{4,3,2,1,0:T(4,128)S(1)}, u32[]{:S(2)}, u32[]{:S(2)}) %all-to-all-start.4) | async-done | bytes 65568 | tf_op jit(solution)/shard_map/all_to_all | solution.py:225
  56.4 0.1 collective-permute-start.1
  56.6 1.6 %collective-permute-start.2 = (f32[1,4,1,2,4,128]{5,4,3,0,1,2:T(4,128)S(1)}, f32[1,4,1,2,4,128]{5,4,3,0,1,2:T(4,128)S(1)}, u32[]{:S(2)}, u32[]{:S(2)}) collective-permute-start(f32[1,4,1,2,4,128]{5,4,3,0,1,2:T(4,128)S(1)} %get-tuple-element.20), channel_id=1, source_target_pairs={{0,3},{1,0},{2,1},{3,2},{4,7},{5,4},{6,5},{7,6},{8,11},{9,8},{10,9... | collective-permute-start | bytes 49160 | tf_op jit(solution)/shard_map/ppermute | solution.py:50
  58.1 1.4 %collective-permute-done = f32[1,4,1,2,4,128]{5,4,3,0,1,2:T(4,128)S(1)} collective-permute-done((f32[1,4,1,2,4,128]{5,4,3,0,1,2:T(4,128)S(1)}, f32[1,4,1,2,4,128]{5,4,3,0,1,2:T(4,128)S(1)}, u32[]{:S(2)}, u32[]{:S(2)}) %collective-permute-start) | collective-permute-done | bytes 16416 | tf_op jit(solution)/shard_map/ppermute | solution.py:50
  59.5 0.7 %collective-permute-done.1 = f32[1,4,1,2,4,128]{5,4,3,0,1,2:T(4,128)S(1)} collective-permute-done((f32[1,4,1,2,4,128]{5,4,3,0,1,2:T(4,128)S(1)}, f32[1,4,1,2,4,128]{5,4,3,0,1,2:T(4,128)S(1)}, u32[]{:S(2)}, u32[]{:S(2)}) %collective-permute-start.1) | collective-permute-done | bytes 16416 | tf_op jit(solution)/shard_map/ppermute | solution.py:50
  60.2 1.2 %gather_fusion.2 = f32[32,4,128]{2,1,0:T(4,128)} fusion(f32[32,4,128]{2,1,0:T(4,128)S(1)} %bitcast.779, s32[1024]{0:T(1024)S(1)} %pad_clamp_fusion), kind=kCustom, calls=%fused_computation.2 | custom fusion | bytes 131200 | tf_op jit(solution)/shard_map/gather | solution.py:233
  (80 shorter events, 2.0 us)
Async XLA Ops:
  0.0 35.1 %copy-start = (f32[64,4,512]{2,1,0:T(4,128)S(1)}, f32[64,4,512]{2,1,0:T(4,128)}, u32[]{:S(2)}) copy-start(f32[64,4,512]{2,1,0:T(4,128)} %param.8) | copy-start | bytes 1572868
  1.7 7.2 %copy-start.3 = (f32[24,64]{1,0:T(8,128)S(1)}, f32[24,64]{1,0:T(8,128)}, u32[]{:S(2)}) copy-start(f32[24,64]{1,0:T(8,128)} %param.9) | copy-start | bytes 18436
  1.7 7.3 %copy-start.7 = (f32[8]{0:T(128)S(1)}, f32[8]{0:T(128)}, u32[]{:S(2)}) copy-start(f32[8]{0:T(128)} %constant.131) | copy-start | bytes 100
  1.7 7.3 %copy-start.8 = (f32[8]{0:T(128)S(1)}, f32[8]{0:T(128)}, u32[]{:S(2)}) copy-start(f32[8]{0:T(128)} %constant.129.clone) | copy-start | bytes 100
  2.4 6.7 %copy-start.1 = (f32[3,4096]{1,0:T(4,128)S(1)}, f32[3,4096]{1,0:T(4,128)}, u32[]{:S(2)}) copy-start(f32[3,4096]{1,0:T(4,128)} %param.10) | copy-start | bytes 147460
  2.4 12.1 %all-to-all-start = ((s32[4,4,2]{1,2,0:T(2,128)}), s32[4,4,2]{1,2,0:T(2,128)S(1)}, u32[]{:S(2)}, u32[]{:S(2)}) async-start(s32[4,4,2]{1,2,0:T(2,128)} %copy.171), calls=%async_computation | async-start | bytes 8192 | tf_op jit(solution)/shard_map/all_to_all | solution.py:204
  15.2 7.0 %all-to-all-start.1 = ((s32[4,4,2]{0,2,1:T(2,128)}), s32[4,4,2]{0,2,1:T(2,128)S(1)}, u32[]{:S(2)}, u32[]{:S(2)}) async-start(s32[4,4,2]{0,2,1:T(2,128)} %copy.172), calls=%async_computation.1 | async-start | bytes 8192 | tf_op jit(solution)/shard_map/all_to_all | solution.py:203
  22.1 8.9 %all-to-all-start.2 = ((f32[4,4,2,3,128]{4,2,1,3,0:T(2,128)}), f32[4,4,2,3,128]{4,2,1,3,0:T(2,128)S(1)}, u32[]{:S(2)}, u32[]{:S(2)}) async-start(f32[4,4,2,3,128]{4,2,1,3,0:T(2,128)} %copy.180), calls=%async_computation.2 | async-start | bytes 98304 | tf_op jit(solution)/shard_map/all_to_all | solution.py:191
  26.2 0.7 %copy-start.4 = (f32[2,128]{1,0:T(2,128)S(1)}, f32[2,128]{1,0:T(2,128)}, u32[]{:S(2)}) copy-start(f32[2,128]{1,0:T(2,128)} %constant.117.clone.1) | copy-start | bytes 3076
  26.9 0.7 %copy-start.6 = (f32[24]{0:T(128)S(1)}, f32[24]{0:T(128)}, u32[]{:S(2)}) copy-start(f32[24]{0:T(128)} %constant.130) | copy-start | bytes 292
  28.3 0.7 %copy-start.5 = (f32[3,8]{1,0:T(4,128)S(1)}, f32[3,8]{1,0:T(4,128)}, u32[]{:S(2)}) copy-start(f32[3,8]{1,0:T(4,128)} %constant.128.clone) | copy-start | bytes 292
  31.7 7.3 %all-to-all-start.3 = ((f32[4,4,2,3,128]{4,2,0,3,1:T(2,128)}), f32[4,4,2,3,128]{4,2,0,3,1:T(2,128)S(1)}, u32[]{:S(2)}, u32[]{:S(2)}) async-start(f32[4,4,2,3,128]{4,2,0,3,1:T(2,128)} %copy.181), calls=%async_computation.3 | async-start | bytes 98304 | tf_op jit(solution)/shard_map/all_to_all | solution.py:190
  39.6 0.7 %copy-start.2 = (f32[2,128]{1,0:T(2,128)S(1)}, f32[2,128]{1,0:T(2,128)}, u32[]{:S(2)}) copy-start(f32[2,128]{1,0:T(2,128)} %constant.122.clone.1) | copy-start | bytes 3076
  47.3 9.0 %all-to-all-start.4 = ((f32[4,4,2,4,128]{4,3,2,1,0:T(4,128)}), f32[4,4,2,4,128]{4,3,2,1,0:T(4,128)S(1)}, u32[]{:S(2)}, u32[]{:S(2)}) async-start(f32[4,4,2,4,128]{4,3,2,1,0:T(4,128)} %broadcast_select_fusion), calls=%async_computation.4 | async-start | bytes 131072 | tf_op jit(solution)/shard_map/all_to_all | solution.py:225
  56.3 3.2 %collective-permute-start = (f32[1,4,1,2,4,128]{5,4,3,0,1,2:T(4,128)S(1)}, f32[1,4,1,2,4,128]{5,4,3,0,1,2:T(4,128)S(1)}, u32[]{:S(2)}, u32[]{:S(2)}) collective-permute-start(f32[1,4,1,2,4,128]{5,4,3,0,1,2:T(4,128)S(1)} %get-tuple-element.22), channel_id=1, source_target_pairs={{0,1},{1,2},{2,3},{3,0},{4,5},{5,6},{6,7},{7,4},{8,9},{9,10},{10,1... | collective-permute-start | bytes 49160 | tf_op jit(solution)/shard_map/ppermute | solution.py:50
  56.4 3.8 %collective-permute-start.1 = (f32[1,4,1,2,4,128]{5,4,3,0,1,2:T(4,128)S(1)}, f32[1,4,1,2,4,128]{5,4,3,0,1,2:T(4,128)S(1)}, u32[]{:S(2)}, u32[]{:S(2)}) collective-permute-start(f32[1,4,1,2,4,128]{5,4,3,0,1,2:T(4,128)S(1)} %get-tuple-element.21), channel_id=1, source_target_pairs={{0,2},{1,3},{2,0},{3,1},{4,6},{5,7},{6,4},{7,5},{8,10},{9,11},{10,... | collective-permute-start | bytes 49160 | tf_op jit(solution)/shard_map/ppermute | solution.py:50
  56.6 3.7 %collective-permute-start.2 = (f32[1,4,1,2,4,128]{5,4,3,0,1,2:T(4,128)S(1)}, f32[1,4,1,2,4,128]{5,4,3,0,1,2:T(4,128)S(1)}, u32[]{:S(2)}, u32[]{:S(2)}) collective-permute-start(f32[1,4,1,2,4,128]{5,4,3,0,1,2:T(4,128)S(1)} %get-tuple-element.20), channel_id=1, source_target_pairs={{0,3},{1,0},{2,1},{3,2},{4,7},{5,4},{6,5},{7,6},{8,11},{9,8},{10,9... | collective-permute-start | bytes 49160 | tf_op jit(solution)/shard_map/ppermute | solution.py:50
